TPU v7x, 32 devices: a whole 2x2x4 slice. The times are simulated.
32 devices in a mesh: grp: 2 (over x), dev: 16 (over z, y, core).
Axes of the slice: x: 2, y: 2, z: 4, core: 2. Of those that a mesh axis runs over, the one named last changes fastest.
Arguments:
- query: bfloat16 [64, 128, 4096], P(('grp', 'dev')), may hold values from -100 to 100
- grad_out: bfloat16 [64, 128, 4096], P(('grp', 'dev')), may hold values from -6 to 6
- branch_kv: bfloat16 [64, 128, 1024], P(('grp', 'dev')), may hold values from -6 to 6
- root_kv: bfloat16 [1024, 1024], P('dev'), may hold values from -24 to 24
- lengths: int32 [64], P(('grp', 'dev')), may hold values from 0 to 128, as said below
- segments: int32 [64], P(('grp', 'dev')), may hold values from 0 to 3
Outputs:
- query_grad: bfloat16 [64, 128, 4096], P(('grp', 'dev'))
- branch_grad: bfloat16 [64, 128, 1024], P(('grp', 'dev'))
- root_grad: float32 [1024, 1024], P('dev')
Inputs may be any that keep to these rules, and one draw needn't show every extreme that they name: `lengths`: A slot with length 0 holds no branch. A device's slots with live positions come before its empty slots. Within a group, device d and device d + 16/2 (d < 8) hold exactly 2 slots with live positions together; a quarter of a group's devices hold 2 such slots and a quarter hold none.
All inputs are finite; a program needn't handle non-finite values.
Results may differ from a plain program's by a relative error of at most 0.0069.
Values may be sent and summed in bfloat16 or wider, within the bound.
No kernel may reach another device: no remote copies, remote signals or barrier semaphores. Data moves between devices by JAX's collectives and lax.ppermute only.
A program may use at most 128 MiB of HBM per device.

v0:
```python
import jax
import jax.numpy as jnp
from jax import lax
from jax.sharding import PartitionSpec as P

H = 32
KVH = 4
DH = 128
SEGS = 4


def passed_along(block, axis, distance):
    devices = range(lax.axis_size(axis))
    route = [((i - distance) % len(devices), i) for i in devices]
    return lax.ppermute(block, axis, route)


def tile_grads(query, grad, branch, length, segment, root_keys):
    rows = query.shape[0]
    width = KVH * DH
    groups = H // KVH
    roots = root_keys.shape[0]
    everything = jnp.concatenate([root_keys, branch], axis=0)
    span = roots + rows
    scale = DH ** (-0.5)
    row_pos = lax.broadcasted_iota(jnp.int32, (rows, span), 0)
    col_pos = lax.broadcasted_iota(jnp.int32, (rows, span), 1)
    visible = jnp.where(
        col_pos < roots, col_pos < (segment + 1) * (roots // SEGS), col_pos - roots <= row_pos
    )
    live = lax.broadcasted_iota(jnp.int32, (rows, 1), 0) < length
    grad = jnp.where(live, grad, jnp.zeros_like(grad))
    dq_parts = []
    dk_parts = []
    dv_parts = []
    for head in range(KVH):
        q_head = query[:, head * groups * DH : (head + 1) * groups * DH].reshape(rows, groups, DH)
        g_head = grad[:, head * groups * DH : (head + 1) * groups * DH].reshape(rows, groups, DH)
        k_head = everything[:, head * DH : (head + 1) * DH]
        v_head = everything[:, width + head * DH : width + (head + 1) * DH]
        scores = (
            jnp.einsum("tgd,ld->gtl", q_head, k_head, preferred_element_type=jnp.float32) * scale
        )
        scores = jnp.where(visible[None], scores, jnp.float32(-1e30))
        peak = jnp.max(scores, axis=-1, keepdims=True)
        weights = jnp.exp(scores - peak)
        weights = weights / jnp.sum(weights, axis=-1, keepdims=True)
        probs = weights.astype(jnp.bfloat16)
        output = jnp.einsum("gtl,ld->tgd", probs, v_head, preferred_element_type=jnp.float32)
        delta = jnp.sum(g_head.astype(jnp.float32) * output, axis=-1)
        dv_parts.append(
            jnp.einsum("gtl,tgd->ld", probs, g_head, preferred_element_type=jnp.float32)
        )
        prob_grad = jnp.einsum("tgd,ld->gtl", g_head, v_head, preferred_element_type=jnp.float32)
        score_grad = (weights * (prob_grad - delta.T[:, :, None]) * scale).astype(jnp.bfloat16)
        dq_parts.append(
            jnp.einsum(
                "gtl,ld->tgd", score_grad, k_head, preferred_element_type=jnp.float32
            ).reshape(rows, groups * DH)
        )
        dk_parts.append(
            jnp.einsum("gtl,tgd->ld", score_grad, q_head, preferred_element_type=jnp.float32)
        )
    dq = jnp.concatenate(dq_parts, axis=1).astype(jnp.bfloat16)
    dkv = jnp.concatenate(dk_parts + dv_parts, axis=1)
    return (dq, dkv[roots:].astype(jnp.bfloat16), dkv[:roots])


def local(query, grad_out, branch_kv, root_kv, lengths, segments):
    root_keys = lax.all_gather(root_kv, "dev", axis=0, tiled=True)
    half = lax.axis_size("dev") // 2
    live_count = jnp.sum((lengths > 0).astype(jnp.int32))
    arrived = passed_along(
        (query[1], grad_out[1], branch_kv[1], lengths[1:], segments[1:]), "dev", half
    )
    resident = live_count > 0
    q_tile = jnp.where(resident, query[0], arrived[0])
    g_tile = jnp.where(resident, grad_out[0], arrived[1])
    b_tile = jnp.where(resident, branch_kv[0], arrived[2])
    length = jnp.where(resident, lengths[0], arrived[3][0])
    segment = jnp.where(resident, segments[0], arrived[4][0])
    dq, dbranch, total = tile_grads(q_tile, g_tile, b_tile, length, segment, root_keys)
    returned = passed_along((dq, dbranch), "dev", half)
    second = live_count > 1
    query_grad = jnp.stack(
        [
            jnp.where(resident, dq, jnp.zeros_like(dq)),
            jnp.where(second, returned[0], jnp.zeros_like(dq)),
        ]
    )
    branch_grad = jnp.stack(
        [
            jnp.where(resident, dbranch, jnp.zeros_like(dbranch)),
            jnp.where(second, returned[1], jnp.zeros_like(dbranch)),
        ]
    )
    within = lax.psum_scatter(total, "dev", scatter_dimension=0, tiled=True)
    root_grad = lax.psum(within, "grp")
    return (query_grad, branch_grad, root_grad)


def solution(mesh):
    placed = (
        P(("grp", "dev"), None, None),
        P(("grp", "dev"), None, None),
        P(("grp", "dev"), None, None),
        P("dev", None),
        P(("grp", "dev")),
        P(("grp", "dev")),
    )
    return jax.shard_map(
        local,
        mesh=mesh,
        in_specs=placed,
        out_specs=(P(("grp", "dev"), None, None), P(("grp", "dev"), None, None), P("dev", None)),
        check_vma=False,
    )
```

profile of v0, /device:TPU:0, one launch (start us, length us, event | category | flops | bytes accessed | tf_op | source)
XLA Modules:
  0.0 334.5 jit_solution(13698584150056525036)
XLA Ops:
  9.6 4.1 %collective-permute-start = (bf16[128,1024]{1,0:T(8,128)(2,1)}, bf16[128,1024]{1,0:T(8,128)(2,1)}, u32[]{:S(2)}, u32[]{:S(2)}) collective-permute-start(bf16[128,1024]{1,0:T(8,128)(2,1)} %slice_bitcast_fusion), channel_id=1, source_target_pairs={{8,0},{9,1},{10,2},{11,3},{12,4},{13,5},{14,6},{15,7},{0,8},{1,9},... | collective-permute-start | bytes 786440 | tf_op jit(solution)/shard_map/ppermute | solution.py:15
  17.3 2.9 collective-permute-start.3
  23.9 2.9 collective-permute-start.2
  29.5 69.0 %collective-permute-done.1 = s32[1]{0:T(128)} collective-permute-done((s32[1]{0:T(128)}, s32[1]{0:T(128)}, u32[]{:S(2)}, u32[]{:S(2)}) %collective-permute-start.1) | collective-permute-done | bytes 36 | tf_op jit(solution)/shard_map/ppermute | solution.py:15
  104.4 15.7 %collective-permute-done.2 = bf16[128,4096]{0,1:T(8,128)(2,1)} collective-permute-done((bf16[128,4096]{0,1:T(8,128)(2,1)}, bf16[128,4096]{0,1:T(8,128)(2,1)}, u32[]{:S(2)}, u32[]{:S(2)}) %collective-permute-start.2) | collective-permute-done | bytes 1048608 | tf_op jit(solution)/shard_map/ppermute | solution.py:15
  121.1 22.5 %all-gather.2.cloned.1.call-done = bf16[1024,1024]{1,0:T(8,128)(2,1)} async-done(((bf16[64,1024]{1,0:T(8,128)(2,1)}), bf16[1024,1024]{1,0:T(8,128)(2,1)}) %all-gather.2.cloned.1.call-update) | async-done | bytes 2097168 | tf_op jit(solution)/shard_map/all_gather | solution.py:70
  143.6 2.2 fusion.47
  145.9 3.8 %exponential_reduce_fusion.3 = (f32[8,128]{1,0:T(8,128)S(1)}, f32[8,128,1152]{1,2,0:T(8,128)}) fusion(pred[128,1152]{0,1:T(8,128)(4,1)S(1)} %fusion.45, bf16[128,8,128]{0,2,1:T(8,128)(2,1)S(1)} %bitcast.304, bf16[1152,128]{1,0:T(8,128)(2,1)S(1)} %get-tuple-element.8), kind=kOutput, calls=%fused_computation.50 | convolution fusion | flops 306709632 | bytes 5427200 | tf_op jit(solution)/shard_map/sub | solution.py:46
  149.7 3.1 fusion.40
  154.2 1.8 copy-done.16
  159.0 4.4 %exponential_reduce_fusion = (f32[8,128]{1,0:T(8,128)}, f32[8,128,1152]{1,2,0:T(8,128)}) fusion(pred[128,1152]{0,1:T(8,128)(4,1)S(1)} %fusion.45, bf16[128,8,128]{0,2,1:T(8,128)(2,1)S(1)} %bitcast.298, bf16[1152,128]{1,0:T(8,128)(2,1)S(1)} %get-tuple-element.12), kind=kOutput, calls=%fused_computation.44 | convolution fusion | flops 306709632 | bytes 5427200 | tf_op jit(solution)/shard_map/sub | solution.py:46
  163.4 3.1 fusion.43
  168.1 2.7 fusion.10
  170.9 5.5 %exponential_reduce_fusion.1 = (f32[8,128]{1,0:T(8,128)}, f32[8,128,1152]{1,2,0:T(8,128)}) fusion(pred[128,1152]{0,1:T(8,128)(4,1)S(1)} %fusion.45, bf16[128,8,128]{0,2,1:T(8,128)(2,1)} %bitcast.300, bf16[1152,128]{1,0:T(8,128)(2,1)} %get-tuple-element.10), kind=kOutput, calls=%fused_computation.46 | convolution fusion | flops 306709632 | bytes 5427200 | tf_op jit(solution)/shard_map/sub | solution.py:46
  176.3 4.4 %fusion.42 = bf16[8,128,1152]{1,2,0:T(8,128)(2,1)} fusion(f32[8,128]{1,0:T(8,128)} %get-tuple-element.31, f32[8,128,1152]{1,2,0:T(8,128)} %get-tuple-element.32), kind=kLoop, calls=%fused_computation.78 | loop fusion | flops 2359296 | bytes 7081984 | tf_op jit(solution)/shard_map/convert_element_type | solution.py:48
  180.7 5.7 %exponential_reduce_fusion.2 = (f32[8,128]{1,0:T(8,128)}, f32[8,128,1152]{1,2,0:T(8,128)}) fusion(pred[128,1152]{0,1:T(8,128)(4,1)S(1)} %fusion.45, bf16[128,8,128]{0,2,1:T(8,128)(2,1)} %bitcast.302, bf16[1152,128]{1,0:T(8,128)(2,1)} %get-tuple-element.9), kind=kOutput, calls=%fused_computation.48 | convolution fusion | flops 306709632 | bytes 5427200 | tf_op jit(solution)/shard_map/sub | solution.py:46
  186.4 3.1 fusion.41
  206.1 2.1 copy-done.12
  208.2 2.3 slice.136
  212.8 2.4 convolution_convert_fusion.1
  218.3 2.4 collective-permute-start.6
  220.9 80.7 %collective-permute-done.6 = bf16[128,1024]{1,0:T(8,128)(2,1)S(1)} collective-permute-done((bf16[128,1024]{1,0:T(8,128)(2,1)S(1)}, bf16[128,1024]{1,0:T(8,128)(2,1)S(1)}, u32[]{:S(2)}, u32[]{:S(2)}) %collective-permute-start.6) | collective-permute-done | bytes 262176 | tf_op jit(solution)/shard_map/ppermute | solution.py:15
  304.9 2.7 copy.105
  307.6 18.6 %all-reduce.2.cloned.1.call-done = f32[64,1024]{1,0:T(8,128)} async-done(((f32[64,1024]{1,0:T(8,128)}), f32[64,1024]{1,0:T(8,128)}) %all-reduce.2.cloned.1.call-update) | async-done | bytes 262160 | tf_op jit(solution)/shard_map/psum | solution.py:98
  (137 shorter events, 47.9 us)
Async XLA Ops:
  7.2 136.5 %all-gather.2.cloned.1.call-start = ((), (), s32[]{:S(2)}) async-start(), calls=%async_computation.1 | async-start | bytes 2228224 | tf_op jit(solution)/shard_map/all_gather | solution.py:70
  7.9 295.6 %reduce-scatter.2.cloned.1.call-start = ((), (), s32[]{:S(2)}) async-start(), calls=%async_computation.2 | async-start | bytes 4456448 | tf_op jit(solution)/shard_map/reduce_scatter | solution.py:97
  9.6 7.1 %copy-start.34 = (s32[2]{0:T(128)S(1)}, s32[2]{0:T(128)}, u32[]{:S(2)}) copy-start(s32[2]{0:T(128)} %param.10) | copy-start | bytes 28
  9.6 10.6 %copy-start.33 = (s32[2]{0:T(128)S(1)}, s32[2]{0:T(128)}, u32[]{:S(2)}) copy-start(s32[2]{0:T(128)} %param.11) | copy-start | bytes 28
  9.6 92.8 %collective-permute-start = (bf16[128,1024]{1,0:T(8,128)(2,1)}, bf16[128,1024]{1,0:T(8,128)(2,1)}, u32[]{:S(2)}, u32[]{:S(2)}) collective-permute-start(bf16[128,1024]{1,0:T(8,128)(2,1)} %slice_bitcast_fusion), channel_id=1, source_target_pairs={{8,0},{9,1},{10,2},{11,3},{12,4},{13,5},{14,6},{15,7},{0,8},{1,9},... | collective-permute-start | bytes 786440 | tf_op jit(solution)/shard_map/ppermute | solution.py:15
  16.7 86.7 %collective-permute-start.4 = (bf16[128,4096]{0,1:T(8,128)(2,1)}, bf16[128,4096]{0,1:T(8,128)(2,1)}, u32[]{:S(2)}, u32[]{:S(2)}) collective-permute-start(bf16[128,4096]{0,1:T(8,128)(2,1)} %bitcast.14), channel_id=1, source_target_pairs={{8,0},{9,1},{10,2},{11,3},{12,4},{13,5},{14,6},{15,7},{0,8},{1,9},... | collective-permute-start | bytes 3145736 | tf_op jit(solution)/shard_map/ppermute | solution.py:15
  17.3 83.8 %collective-permute-start.3 = (s32[1]{0:T(128)}, s32[1]{0:T(128)}, u32[]{:S(2)}, u32[]{:S(2)}) collective-permute-start(s32[1]{0:T(128)} %get-tuple-element.27), channel_id=1, source_target_pairs={{8,0},{9,1},{10,2},{11,3},{12,4},{13,5},{14,6},{15,7},{0,8},{1,9},... | collective-permute-start | bytes 20 | tf_op jit(solution)/shard_map/ppermute | solution.py:15
  20.8 77.6 %collective-permute-start.1 = (s32[1]{0:T(128)}, s32[1]{0:T(128)}, u32[]{:S(2)}, u32[]{:S(2)}) collective-permute-start(s32[1]{0:T(128)} %get-tuple-element.25), channel_id=1, source_target_pairs={{8,0},{9,1},{10,2},{11,3},{12,4},{13,5},{14,6},{15,7},{0,8},{1,9},... | collective-permute-start | bytes 20 | tf_op jit(solution)/shard_map/ppermute | solution.py:15
  23.9 96.2 %collective-permute-start.2 = (bf16[128,4096]{0,1:T(8,128)(2,1)}, bf16[128,4096]{0,1:T(8,128)(2,1)}, u32[]{:S(2)}, u32[]{:S(2)}) collective-permute-start(bf16[128,4096]{0,1:T(8,128)(2,1)} %bitcast.295), channel_id=1, source_target_pairs={{8,0},{9,1},{10,2},{11,3},{12,4},{13,5},{14,6},{15,7},{0,8},{1,9},... | collective-permute-start | bytes 3145736 | tf_op jit(solution)/shard_map/ppermute | solution.py:15
  103.5 16.7 %copy-start.13 = (bf16[128,4096]{0,1:T(8,128)(2,1)}, bf16[128,4096]{0,1:T(8,128)(2,1)S(1)}, u32[]{:S(2)}) copy-start(bf16[128,4096]{0,1:T(8,128)(2,1)S(1)} %fusion.44) | copy-start | bytes 3145732
  121.1 37.9 %copy-start.26 = (bf16[128,1024]{0,1:T(8,128)(2,1)}, bf16[128,1024]{0,1:T(8,128)(2,1)S(1)}, u32[]{:S(2)}) copy-start(bf16[128,1024]{0,1:T(8,128)(2,1)S(1)} %get-tuple-element.18) | copy-start | bytes 786436
  145.9 3.8 %copy-start.17 = (bf16[1152,128]{1,0:T(8,128)(2,1)}, bf16[1152,128]{1,0:T(8,128)(2,1)S(1)}, u32[]{:S(2)}) copy-start(bf16[1152,128]{1,0:T(8,128)(2,1)S(1)} %get-tuple-element.8) | copy-start | bytes 884740
  145.9 13.1 %copy-start.21 = (bf16[1152,128]{1,0:T(8,128)(2,1)}, bf16[1152,128]{1,0:T(8,128)(2,1)S(1)}, u32[]{:S(2)}) copy-start(bf16[1152,128]{1,0:T(8,128)(2,1)S(1)} %get-tuple-element.12) | copy-start | bytes 884740
  149.7 3.1 copy-start.3
  152.8 3.2 copy-start.16
  163.4 3.1 copy-start.23
  163.4 4.7 %copy-start.14 = (f32[8,128,1152]{1,2,0:T(8,128)S(1)}, f32[8,128,1152]{1,2,0:T(8,128)}, u32[]{:S(2)}) copy-start(f32[8,128,1152]{1,2,0:T(8,128)} %get-tuple-element.30) | copy-start | bytes 14155780
  186.4 4.4 %copy-start.15 = (f32[8,128,1152]{1,2,0:T(8,128)S(1)}, f32[8,128,1152]{1,2,0:T(8,128)}, u32[]{:S(2)}) copy-start(f32[8,128,1152]{1,2,0:T(8,128)} %get-tuple-element.34) | copy-start | bytes 14155780
  186.4 4.4 %copy-start.32 = (f32[8,128]{1,0:T(8,128)S(1)}, f32[8,128]{1,0:T(8,128)}, u32[]{:S(2)}) copy-start(f32[8,128]{1,0:T(8,128)} %get-tuple-element.33) | copy-start | bytes 12292
  189.6 7.1 %slice-start.2 = ((s8[4718592]{0:T(1024)(128)(4,1)}), s8[4194304]{0:T(1024)(128)(4,1)S(1)}, s32[]{:S(2)}) async-start(s8[4718592]{0:T(1024)(128)(4,1)} %bitcast.276), calls=%async_computation.6 | async-start | bytes 8388608
  190.8 5.8 %slice-start.3 = ((s8[4718592]{0:T(1024)(128)(4,1)}), s8[524288]{0:T(1024)(128)(4,1)S(1)}, s32[]{:S(2)}) async-start(s8[4718592]{0:T(1024)(128)(4,1)} %bitcast.276), calls=%async_computation.7 | async-start | bytes 1048576
  210.6 115.7 %all-reduce.2.cloned.1.call-start = ((), (), s32[]{:S(2)}) async-start(), calls=%async_computation.3 | async-start | bytes 524288 | tf_op jit(solution)/shard_map/psum | solution.py:98
  216.5 85.9 %collective-permute-start.5 = (bf16[128,4096]{0,1:T(8,128)(2,1)S(1)}, bf16[128,4096]{0,1:T(8,128)(2,1)S(1)}, u32[]{:S(2)}, u32[]{:S(2)}) collective-permute-start(bf16[128,4096]{0,1:T(8,128)(2,1)S(1)} %pad_maximum_fusion.1), channel_id=1, source_target_pairs={{8,0},{9,1},{10,2},{11,3},{12,4},{13,5},{14,6},{15,7},{0,8},{1,9},... | collective-permute-start | bytes 3145736 | tf_op jit(solution)/shard_map/ppermute | solution.py:15
  218.3 83.3 %collective-permute-start.6 = (bf16[128,1024]{1,0:T(8,128)(2,1)S(1)}, bf16[128,1024]{1,0:T(8,128)(2,1)S(1)}, u32[]{:S(2)}, u32[]{:S(2)}) collective-permute-start(bf16[128,1024]{1,0:T(8,128)(2,1)S(1)} %get-tuple-element.7), channel_id=1, source_target_pairs={{8,0},{9,1},{10,2},{11,3},{12,4},{13,5},{14,6},{15,7},{0,8},{1,9},... | collective-permute-start | bytes 786440 | tf_op jit(solution)/shard_map/ppermute | solution.py:15
  (25 other events, 52.1 us)
Sparse Core Ops, SparseCore 0:
  10.1 133.4 all-gather.1
  210.7 85.1 reduce-scatter.1
  303.6 22.6 all-reduce.1
where the time goes:
time: 335 us; the launch traced here: 334 us
  waiting for transfers between devices  207 us (62%)
  matrix products  40.4 us (12%)
  local copies, waits for them, and re-layouts  31.2 us (9%)
  other arithmetic  23.9 us (7%)
  between operations  18.4 us (5%)
  starting transfers between devices  13.3 us (4%)
    ppermute x7, waiting for transfers between devices, passed_along(): return lax.ppermute(block, axis, route)  165 us
    all_gather x1, waiting for transfers between devices, local(): root_keys = lax.all_gather(root_kv, 'dev', axis=0, tiled=True)  22.5 us
    unnamed x84, local copies, waits for them, and re-layouts  20.9 us
    sub x4, matrix products, tile_grads(): weights = jnp.exp(scores - peak)  19.4 us
    psum x1, waiting for transfers between devices, local(): root_grad = lax.psum(within, 'grp')  18.6 us
    convert_element_type x4, other arithmetic, tile_grads(): probs = weights.astype(jnp.bfloat16)  13.7 us
    ppermute x7, starting transfers between devices, passed_along(): return lax.ppermute(block, axis, route)  12.9 us
    dot_general x4, matrix products, tile_grads(): jnp.einsum('tgd,ld->gtl', g_head, v_head, preferred_element_type=jnp.floa...  6.71 us
  transfers between devices with their start and end apart: 10, of which 5 were waited for; matrix products, arithmetic and copies ran while one was open for 8% of the time, Pallas kernels for 0%

commit v1 on v0

--- a/solution.py
+++ b/solution.py
@@ -67,7 +67,12 @@
 
 
 def local(query, grad_out, branch_kv, root_kv, lengths, segments):
-    root_keys = lax.all_gather(root_kv, "dev", axis=0, tiled=True)
+    ring = [root_kv]
+    for hop in range(15):
+        ring.append(lax.ppermute(ring[-1], "dev", [(dev, (dev + 1) % 16) for dev in range(16)]))
+    root_keys = jnp.roll(
+        jnp.concatenate(ring[::-1], axis=0), (lax.axis_index("dev") + 1) * ring[0].shape[0], axis=0
+    )
     half = lax.axis_size("dev") // 2
     live_count = jnp.sum((lengths > 0).astype(jnp.int32))
     arrived = passed_along(

time: 335 us -> 378 us (1.13)
  starting transfers between devices: 13.3 us -> 71.1 us
  waiting for transfers between devices: 207 us -> 192 us
    ppermute x7, waiting for transfers between devices: 165 us -> 55.5 us  [passed_along(): return lax.ppermute(block, axis, route)]
    ppermute x0 -> x15, waiting for transfers between devices: none -> 97.5 us  [local(): lax.ppermute(ring[-1], 'dev', [(dev, (dev + 1) % 16) for dev in range(16)])]
    ppermute x7, starting transfers between devices: 12.9 us -> 70.1 us  [passed_along(): return lax.ppermute(block, axis, route)]
    all_gather x1 -> x0, waiting for transfers between devices: 22.5 us -> none  [local(): root_keys = lax.all_gather(root_kv, 'dev', axis=0, tiled=True)]
    reduce_scatter x1, waiting for transfers between devices: 0.01 us -> 19 us  [local(): within = lax.psum_scatter(total, 'dev', scatter_dimension=0, tiled=True)]
    unnamed x84 -> x169, local copies, waits for them, and re-layouts: 20.9 us -> 18 us
  transfers between devices with their start and end apart: 10 -> 24, of which waited for: 5 -> 16; matrix products, arithmetic and copies ran while one was open for 8% -> 8% of each run, Pallas kernels for 0% -> 0%
where the time goes in v1:
time: 378 us; the launch traced here: 377 us
  waiting for transfers between devices  192 us (51%)
  starting transfers between devices  71.1 us (19%)
  matrix products  42.2 us (11%)
  local copies, waits for them, and re-layouts  30.6 us (8%)
  other arithmetic  22.1 us (6%)
  between operations  19 us (5%)
    ppermute x15, waiting for transfers between devices, local(): lax.ppermute(ring[-1], 'dev', [(dev, (dev + 1) % 16) for dev in range(16)])  97.5 us
    ppermute x7, starting transfers between devices, passed_along(): return lax.ppermute(block, axis, route)  70.1 us
    ppermute x7, waiting for transfers between devices, passed_along(): return lax.ppermute(block, axis, route)  55.5 us
    psum x1, waiting for transfers between devices, local(): root_grad = lax.psum(within, 'grp')  20.4 us
    sub x4, matrix products, tile_grads(): weights = jnp.exp(scores - peak)  20.1 us
    reduce_scatter x1, waiting for transfers between devices, local(): within = lax.psum_scatter(total, 'dev', scatter_dimension=0, tiled=True)  19 us
    unnamed x169, local copies, waits for them, and re-layouts  18 us
    convert_element_type x4, other arithmetic, tile_grads(): probs = weights.astype(jnp.bfloat16)  12.7 us
  transfers between devices with their start and end apart: 24, of which 16 were waited for; matrix products, arithmetic and copies ran while one was open for 8% of the time, Pallas kernels for 0%

profile of v1, /device:TPU:0, one launch (start us, length us, event | category | flops | bytes accessed | tf_op | source)
XLA Modules:
  0.0 377.4 jit_solution(9805400605585800686)
XLA Ops:
  7.8 7.8 %collective-permute-done = bf16[64,1024]{1,0:T(8,128)(2,1)S(1)} collective-permute-done((bf16[64,1024]{1,0:T(8,128)(2,1)}, bf16[64,1024]{1,0:T(8,128)(2,1)S(1)}, u32[]{:S(2)}, u32[]{:S(2)}) %collective-permute-start) | collective-permute-done | bytes 131104 | tf_op jit(solution)/shard_map/ppermute | solution.py:72
  15.6 7.1 %collective-permute-done.1 = bf16[64,1024]{1,0:T(8,128)(2,1)S(1)} collective-permute-done((bf16[64,1024]{1,0:T(8,128)(2,1)S(1)}, bf16[64,1024]{1,0:T(8,128)(2,1)S(1)}, u32[]{:S(2)}, u32[]{:S(2)}) %collective-permute-start.1) | collective-permute-done | bytes 131104 | tf_op jit(solution)/shard_map/ppermute | solution.py:72
  23.4 7.1 %collective-permute-done.2 = bf16[64,1024]{1,0:T(8,128)(2,1)S(1)} collective-permute-done((bf16[64,1024]{1,0:T(8,128)(2,1)S(1)}, bf16[64,1024]{1,0:T(8,128)(2,1)S(1)}, u32[]{:S(2)}, u32[]{:S(2)}) %collective-permute-start.2) | collective-permute-done | bytes 131104 | tf_op jit(solution)/shard_map/ppermute | solution.py:72
  31.1 7.1 %collective-permute-done.3 = bf16[64,1024]{1,0:T(8,128)(2,1)S(1)} collective-permute-done((bf16[64,1024]{1,0:T(8,128)(2,1)S(1)}, bf16[64,1024]{1,0:T(8,128)(2,1)S(1)}, u32[]{:S(2)}, u32[]{:S(2)}) %collective-permute-start.3) | collective-permute-done | bytes 131104 | tf_op jit(solution)/shard_map/ppermute | solution.py:72
  38.8 7.1 %collective-permute-done.4 = bf16[64,1024]{1,0:T(8,128)(2,1)S(1)} collective-permute-done((bf16[64,1024]{1,0:T(8,128)(2,1)S(1)}, bf16[64,1024]{1,0:T(8,128)(2,1)S(1)}, u32[]{:S(2)}, u32[]{:S(2)}) %collective-permute-start.4) | collective-permute-done | bytes 131104 | tf_op jit(solution)/shard_map/ppermute | solution.py:72
  56.2 4.1 %collective-permute-done.6 = bf16[64,1024]{1,0:T(8,128)(2,1)S(1)} collective-permute-done((bf16[64,1024]{1,0:T(8,128)(2,1)S(1)}, bf16[64,1024]{1,0:T(8,128)(2,1)S(1)}, u32[]{:S(2)}, u32[]{:S(2)}) %collective-permute-start.6) | collective-permute-done | bytes 131104 | tf_op jit(solution)/shard_map/ppermute | solution.py:72
  64.3 42.3 %collective-permute-start.19 = (bf16[128,4096]{0,1:T(8,128)(2,1)}, bf16[128,4096]{0,1:T(8,128)(2,1)}, u32[]{:S(2)}, u32[]{:S(2)}) collective-permute-start(bf16[128,4096]{0,1:T(8,128)(2,1)} %bitcast.14), channel_id=1, source_target_pairs={{8,0},{9,1},{10,2},{11,3},{12,4},{13,5},{14,6},{15,7},{0,8},{1,9},... | collective-permute-start | bytes 3145736 | tf_op jit(solution)/shard_map/ppermute | solution.py:15
  107.4 25.5 %collective-permute-done.8 = bf16[64,1024]{1,0:T(8,128)(2,1)S(1)} collective-permute-done((bf16[64,1024]{1,0:T(8,128)(2,1)S(1)}, bf16[64,1024]{1,0:T(8,128)(2,1)S(1)}, u32[]{:S(2)}, u32[]{:S(2)}) %collective-permute-start.8) | collective-permute-done | bytes 131104 | tf_op jit(solution)/shard_map/ppermute | solution.py:72
  136.5 21.9 %collective-permute-start.15 = (bf16[128,1024]{1,0:T(8,128)(2,1)}, bf16[128,1024]{1,0:T(8,128)(2,1)S(1)}, u32[]{:S(2)}, u32[]{:S(2)}) collective-permute-start(bf16[128,1024]{1,0:T(8,128)(2,1)} %slice_bitcast_fusion), channel_id=1, source_target_pairs={{8,0},{9,1},{10,2},{11,3},{12,4},{13,5},{14,6},{15,7},{0,8},{1,9},... | collective-permute-start | bytes 786440 | tf_op jit(solution)/shard_map/ppermute | solution.py:15
  162.6 5.2 %collective-permute-done.10 = bf16[64,1024]{1,0:T(8,128)(2,1)S(1)} collective-permute-done((bf16[64,1024]{1,0:T(8,128)(2,1)S(1)}, bf16[64,1024]{1,0:T(8,128)(2,1)S(1)}, u32[]{:S(2)}, u32[]{:S(2)}) %collective-permute-start.10) | collective-permute-done | bytes 131104 | tf_op jit(solution)/shard_map/ppermute | solution.py:72
  168.8 6.0 %collective-permute-done.11 = bf16[64,1024]{1,0:T(8,128)(2,1)S(1)} collective-permute-done((bf16[64,1024]{1,0:T(8,128)(2,1)S(1)}, bf16[64,1024]{1,0:T(8,128)(2,1)S(1)}, u32[]{:S(2)}, u32[]{:S(2)}) %collective-permute-start.11) | collective-permute-done | bytes 131104 | tf_op jit(solution)/shard_map/ppermute | solution.py:72
  175.2 6.7 %collective-permute-done.12 = bf16[64,1024]{1,0:T(8,128)(2,1)S(1)} collective-permute-done((bf16[64,1024]{1,0:T(8,128)(2,1)S(1)}, bf16[64,1024]{1,0:T(8,128)(2,1)S(1)}, u32[]{:S(2)}, u32[]{:S(2)}) %collective-permute-start.12) | collective-permute-done | bytes 131104 | tf_op jit(solution)/shard_map/ppermute | solution.py:72
  182.9 6.1 %collective-permute-done.13 = bf16[64,1024]{1,0:T(8,128)(2,1)S(1)} collective-permute-done((bf16[64,1024]{1,0:T(8,128)(2,1)S(1)}, bf16[64,1024]{1,0:T(8,128)(2,1)S(1)}, u32[]{:S(2)}, u32[]{:S(2)}) %collective-permute-start.13) | collective-permute-done | bytes 131104 | tf_op jit(solution)/shard_map/ppermute | solution.py:72
  190.0 6.1 %collective-permute-done.14 = bf16[64,1024]{1,0:T(8,128)(2,1)S(1)} collective-permute-done((bf16[64,1024]{1,0:T(8,128)(2,1)S(1)}, bf16[64,1024]{1,0:T(8,128)(2,1)S(1)}, u32[]{:S(2)}, u32[]{:S(2)}) %collective-permute-start.14) | collective-permute-done | bytes 131104 | tf_op jit(solution)/shard_map/ppermute | solution.py:72
  198.2 5.5 %exponential_reduce_fusion.3 = (f32[8,128]{1,0:T(8,128)}, f32[8,128,1152]{1,2,0:T(8,128)}) fusion(pred[128,1152]{0,1:T(8,128)(4,1)S(1)} %copy-done.53, bf16[128,8,128]{0,2,1:T(8,128)(2,1)} %bitcast.307, bf16[1152,128]{1,0:T(8,128)(2,1)} %get-tuple-element.8), kind=kOutput, calls=%fused_computation.50 | convolution fusion | flops 306709632 | bytes 5427200 | tf_op jit(solution)/shard_map/sub | solution.py:46
  203.7 3.1 fusion.40
  210.7 5.4 %exponential_reduce_fusion.2 = (f32[8,128]{1,0:T(8,128)}, f32[8,128,1152]{1,2,0:T(8,128)}) fusion(pred[128,1152]{0,1:T(8,128)(4,1)S(1)} %copy-done.53, bf16[128,8,128]{0,2,1:T(8,128)(2,1)} %bitcast.305, bf16[1152,128]{1,0:T(8,128)(2,1)} %get-tuple-element.9), kind=kOutput, calls=%fused_computation.48 | convolution fusion | flops 306709632 | bytes 5427200 | tf_op jit(solution)/shard_map/sub | solution.py:46
  216.1 3.1 fusion.41
  222.9 5.5 %exponential_reduce_fusion.1 = (f32[8,128]{1,0:T(8,128)}, f32[8,128,1152]{1,2,0:T(8,128)}) fusion(pred[128,1152]{0,1:T(8,128)(4,1)S(1)} %copy-done.53, bf16[128,8,128]{0,2,1:T(8,128)(2,1)} %bitcast.303, bf16[1152,128]{1,0:T(8,128)(2,1)} %get-tuple-element.10), kind=kOutput, calls=%fused_computation.46 | convolution fusion | flops 306709632 | bytes 5427200 | tf_op jit(solution)/shard_map/sub | solution.py:46
  228.3 3.3 fusion.42
  237.4 3.8 %exponential_reduce_fusion = (f32[8,128]{1,0:T(8,128)S(1)}, f32[8,128,1152]{1,2,0:T(8,128)}) fusion(pred[128,1152]{0,1:T(8,128)(4,1)S(1)} %copy-done.53, bf16[128,8,128]{0,2,1:T(8,128)(2,1)S(1)} %bitcast.301, bf16[1152,128]{1,0:T(8,128)(2,1)S(1)} %copy-done.21), kind=kOutput, calls=%fused_computation.44 | convolution fusion | flops 306709632 | bytes 5427200 | tf_op jit(solution)/shard_map/sub | solution.py:46
  267.9 55.4 %collective-permute-done.21 = bf16[128,1024]{1,0:T(8,128)(2,1)S(1)} collective-permute-done((bf16[128,1024]{1,0:T(8,128)(2,1)S(1)}, bf16[128,1024]{1,0:T(8,128)(2,1)S(1)}, u32[]{:S(2)}, u32[]{:S(2)}) %collective-permute-start.21) | collective-permute-done | bytes 262176 | tf_op jit(solution)/shard_map/ppermute | solution.py:15
  325.3 19.0 %reduce-scatter.2.cloned.1.call-done = f32[64,1024]{1,0:T(8,128)} async-done(((f32[1024,1024]{1,0:T(8,128)}), f32[64,1024]{1,0:T(8,128)}) %reduce-scatter.2.cloned.1.call-update) | async-done | bytes 262160 | tf_op jit(solution)/shard_map/reduce_scatter | solution.py:102
  348.4 20.4 %all-reduce.2.cloned.1.call-done = f32[64,1024]{1,0:T(8,128)} async-done(((f32[64,1024]{1,0:T(8,128)}), f32[64,1024]{1,0:T(8,128)}) %all-reduce.2.cloned.1.call-update) | async-done | bytes 262160 | tf_op jit(solution)/shard_map/psum | solution.py:103
  (252 shorter events, 73.8 us)
Async XLA Ops:
  7.2 337.1 %reduce-scatter.2.cloned.1.call-start = ((), (), s32[]{:S(2)}) async-start(), calls=%async_computation.1 | async-start | bytes 4456448 | tf_op jit(solution)/shard_map/reduce_scatter | solution.py:102
  7.2 8.4 %collective-permute-start = (bf16[64,1024]{1,0:T(8,128)(2,1)}, bf16[64,1024]{1,0:T(8,128)(2,1)S(1)}, u32[]{:S(2)}, u32[]{:S(2)}) collective-permute-start(bf16[64,1024]{1,0:T(8,128)(2,1)} %param.9), channel_id=1, source_target_pairs={{0,1},{1,2},{2,3},{3,4},{4,5},{5,6},{6,7},{7,8},{8,9},{9,10},{10,1... | collective-permute-start | bytes 393224 | tf_op jit(solution)/shard_map/ppermute | solution.py:72
  15.6 7.1 %collective-permute-start.1 = (bf16[64,1024]{1,0:T(8,128)(2,1)S(1)}, bf16[64,1024]{1,0:T(8,128)(2,1)S(1)}, u32[]{:S(2)}, u32[]{:S(2)}) collective-permute-start(bf16[64,1024]{1,0:T(8,128)(2,1)S(1)} %collective-permute-done), channel_id=1, source_target_pairs={{0,1},{1,2},{2,3},{3,4},{4,5},{5,6},{6,7},{7,8},{8,9},{9,10},{10,1... | collective-permute-start | bytes 393224 | tf_op jit(solution)/shard_map/ppermute | solution.py:72
  23.4 7.1 %collective-permute-start.2 = (bf16[64,1024]{1,0:T(8,128)(2,1)S(1)}, bf16[64,1024]{1,0:T(8,128)(2,1)S(1)}, u32[]{:S(2)}, u32[]{:S(2)}) collective-permute-start(bf16[64,1024]{1,0:T(8,128)(2,1)S(1)} %collective-permute-done.1), channel_id=1, source_target_pairs={{0,1},{1,2},{2,3},{3,4},{4,5},{5,6},{6,7},{7,8},{8,9},{9,10},{10,1... | collective-permute-start | bytes 393224 | tf_op jit(solution)/shard_map/ppermute | solution.py:72
  31.1 7.1 %collective-permute-start.3 = (bf16[64,1024]{1,0:T(8,128)(2,1)S(1)}, bf16[64,1024]{1,0:T(8,128)(2,1)S(1)}, u32[]{:S(2)}, u32[]{:S(2)}) collective-permute-start(bf16[64,1024]{1,0:T(8,128)(2,1)S(1)} %collective-permute-done.2), channel_id=1, source_target_pairs={{0,1},{1,2},{2,3},{3,4},{4,5},{5,6},{6,7},{7,8},{8,9},{9,10},{10,1... | collective-permute-start | bytes 393224 | tf_op jit(solution)/shard_map/ppermute | solution.py:72
  38.8 7.1 %collective-permute-start.4 = (bf16[64,1024]{1,0:T(8,128)(2,1)S(1)}, bf16[64,1024]{1,0:T(8,128)(2,1)S(1)}, u32[]{:S(2)}, u32[]{:S(2)}) collective-permute-start(bf16[64,1024]{1,0:T(8,128)(2,1)S(1)} %collective-permute-done.3), channel_id=1, source_target_pairs={{0,1},{1,2},{2,3},{3,4},{4,5},{5,6},{6,7},{7,8},{8,9},{9,10},{10,1... | collective-permute-start | bytes 393224 | tf_op jit(solution)/shard_map/ppermute | solution.py:72
  45.9 7.2 %collective-permute-start.5 = (bf16[64,1024]{1,0:T(8,128)(2,1)S(1)}, bf16[64,1024]{1,0:T(8,128)(2,1)S(1)}, u32[]{:S(2)}, u32[]{:S(2)}) collective-permute-start(bf16[64,1024]{1,0:T(8,128)(2,1)S(1)} %collective-permute-done.4), channel_id=1, source_target_pairs={{0,1},{1,2},{2,3},{3,4},{4,5},{5,6},{6,7},{7,8},{8,9},{9,10},{10,1... | collective-permute-start | bytes 393224 | tf_op jit(solution)/shard_map/ppermute | solution.py:72
  47.2 114.1 %collective-permute-start.18 = (s32[1]{0:T(128)}, s32[1]{0:T(128)}, u32[]{:S(2)}, u32[]{:S(2)}) collective-permute-start(s32[1]{0:T(128)} %get-tuple-element.27), channel_id=1, source_target_pairs={{8,0},{9,1},{10,2},{11,3},{12,4},{13,5},{14,6},{15,7},{0,8},{1,9},... | collective-permute-start | bytes 20 | tf_op jit(solution)/shard_map/ppermute | solution.py:15
  48.6 88.0 %collective-permute-start.16 = (s32[1]{0:T(128)}, s32[1]{0:T(128)}, u32[]{:S(2)}, u32[]{:S(2)}) collective-permute-start(s32[1]{0:T(128)} %get-tuple-element.25), channel_id=1, source_target_pairs={{8,0},{9,1},{10,2},{11,3},{12,4},{13,5},{14,6},{15,7},{0,8},{1,9},... | collective-permute-start | bytes 20 | tf_op jit(solution)/shard_map/ppermute | solution.py:15
  53.1 7.2 %collective-permute-start.6 = (bf16[64,1024]{1,0:T(8,128)(2,1)S(1)}, bf16[64,1024]{1,0:T(8,128)(2,1)S(1)}, u32[]{:S(2)}, u32[]{:S(2)}) collective-permute-start(bf16[64,1024]{1,0:T(8,128)(2,1)S(1)} %collective-permute-done.5), channel_id=1, source_target_pairs={{0,1},{1,2},{2,3},{3,4},{4,5},{5,6},{6,7},{7,8},{8,9},{9,10},{10,1... | collective-permute-start | bytes 393224 | tf_op jit(solution)/shard_map/ppermute | solution.py:72
  56.2 118.6 %collective-permute-start.17 = (bf16[128,4096]{0,1:T(8,128)(2,1)}, bf16[128,4096]{0,1:T(8,128)(2,1)}, u32[]{:S(2)}, u32[]{:S(2)}) collective-permute-start(bf16[128,4096]{0,1:T(8,128)(2,1)} %bitcast.7), channel_id=1, source_target_pairs={{8,0},{9,1},{10,2},{11,3},{12,4},{13,5},{14,6},{15,7},{0,8},{1,9},... | collective-permute-start | bytes 3145736 | tf_op jit(solution)/shard_map/ppermute | solution.py:15
  60.3 46.3 %collective-permute-start.7 = (bf16[64,1024]{1,0:T(8,128)(2,1)S(1)}, bf16[64,1024]{1,0:T(8,128)(2,1)S(1)}, u32[]{:S(2)}, u32[]{:S(2)}) collective-permute-start(bf16[64,1024]{1,0:T(8,128)(2,1)S(1)} %collective-permute-done.6), channel_id=1, source_target_pairs={{0,1},{1,2},{2,3},{3,4},{4,5},{5,6},{6,7},{7,8},{8,9},{9,10},{10,1... | collective-permute-start | bytes 393224 | tf_op jit(solution)/shard_map/ppermute | solution.py:72
  64.3 110.5 %collective-permute-start.19 = (bf16[128,4096]{0,1:T(8,128)(2,1)}, bf16[128,4096]{0,1:T(8,128)(2,1)}, u32[]{:S(2)}, u32[]{:S(2)}) collective-permute-start(bf16[128,4096]{0,1:T(8,128)(2,1)} %bitcast.14), channel_id=1, source_target_pairs={{8,0},{9,1},{10,2},{11,3},{12,4},{13,5},{14,6},{15,7},{0,8},{1,9},... | collective-permute-start | bytes 3145736 | tf_op jit(solution)/shard_map/ppermute | solution.py:15
  106.6 26.2 %collective-permute-start.8 = (bf16[64,1024]{1,0:T(8,128)(2,1)S(1)}, bf16[64,1024]{1,0:T(8,128)(2,1)S(1)}, u32[]{:S(2)}, u32[]{:S(2)}) collective-permute-start(bf16[64,1024]{1,0:T(8,128)(2,1)S(1)} %collective-permute-done.7), channel_id=1, source_target_pairs={{0,1},{1,2},{2,3},{3,4},{4,5},{5,6},{6,7},{7,8},{8,9},{9,10},{10,1... | collective-permute-start | bytes 393224 | tf_op jit(solution)/shard_map/ppermute | solution.py:72
  132.9 26.8 %collective-permute-start.9 = (bf16[64,1024]{1,0:T(8,128)(2,1)S(1)}, bf16[64,1024]{1,0:T(8,128)(2,1)S(1)}, u32[]{:S(2)}, u32[]{:S(2)}) collective-permute-start(bf16[64,1024]{1,0:T(8,128)(2,1)S(1)} %collective-permute-done.8), channel_id=1, source_target_pairs={{0,1},{1,2},{2,3},{3,4},{4,5},{5,6},{6,7},{7,8},{8,9},{9,10},{10,1... | collective-permute-start | bytes 393224 | tf_op jit(solution)/shard_map/ppermute | solution.py:72
  136.5 31.2 %collective-permute-start.15 = (bf16[128,1024]{1,0:T(8,128)(2,1)}, bf16[128,1024]{1,0:T(8,128)(2,1)S(1)}, u32[]{:S(2)}, u32[]{:S(2)}) collective-permute-start(bf16[128,1024]{1,0:T(8,128)(2,1)} %slice_bitcast_fusion), channel_id=1, source_target_pairs={{8,0},{9,1},{10,2},{11,3},{12,4},{13,5},{14,6},{15,7},{0,8},{1,9},... | collective-permute-start | bytes 786440 | tf_op jit(solution)/shard_map/ppermute | solution.py:15
  159.7 8.1 %collective-permute-start.10 = (bf16[64,1024]{1,0:T(8,128)(2,1)S(1)}, bf16[64,1024]{1,0:T(8,128)(2,1)S(1)}, u32[]{:S(2)}, u32[]{:S(2)}) collective-permute-start(bf16[64,1024]{1,0:T(8,128)(2,1)S(1)} %collective-permute-done.9), channel_id=1, source_target_pairs={{0,1},{1,2},{2,3},{3,4},{4,5},{5,6},{6,7},{7,8},{8,9},{9,10},{10,1... | collective-permute-start | bytes 393224 | tf_op jit(solution)/shard_map/ppermute | solution.py:72
  167.8 7.1 %collective-permute-start.11 = (bf16[64,1024]{1,0:T(8,128)(2,1)S(1)}, bf16[64,1024]{1,0:T(8,128)(2,1)S(1)}, u32[]{:S(2)}, u32[]{:S(2)}) collective-permute-start(bf16[64,1024]{1,0:T(8,128)(2,1)S(1)} %collective-permute-done.10), channel_id=1, source_target_pairs={{0,1},{1,2},{2,3},{3,4},{4,5},{5,6},{6,7},{7,8},{8,9},{9,10},{10,1... | collective-permute-start | bytes 393224 | tf_op jit(solution)/shard_map/ppermute | solution.py:72
  174.8 7.1 %collective-permute-start.12 = (bf16[64,1024]{1,0:T(8,128)(2,1)S(1)}, bf16[64,1024]{1,0:T(8,128)(2,1)S(1)}, u32[]{:S(2)}, u32[]{:S(2)}) collective-permute-start(bf16[64,1024]{1,0:T(8,128)(2,1)S(1)} %collective-permute-done.11), channel_id=1, source_target_pairs={{0,1},{1,2},{2,3},{3,4},{4,5},{5,6},{6,7},{7,8},{8,9},{9,10},{10,1... | collective-permute-start | bytes 393224 | tf_op jit(solution)/shard_map/ppermute | solution.py:72
  181.9 7.1 %collective-permute-start.13 = (bf16[64,1024]{1,0:T(8,128)(2,1)S(1)}, bf16[64,1024]{1,0:T(8,128)(2,1)S(1)}, u32[]{:S(2)}, u32[]{:S(2)}) collective-permute-start(bf16[64,1024]{1,0:T(8,128)(2,1)S(1)} %collective-permute-done.12), channel_id=1, source_target_pairs={{0,1},{1,2},{2,3},{3,4},{4,5},{5,6},{6,7},{7,8},{8,9},{9,10},{10,1... | collective-permute-start | bytes 393224 | tf_op jit(solution)/shard_map/ppermute | solution.py:72
  189.0 7.1 %collective-permute-start.14 = (bf16[64,1024]{1,0:T(8,128)(2,1)S(1)}, bf16[64,1024]{1,0:T(8,128)(2,1)S(1)}, u32[]{:S(2)}, u32[]{:S(2)}) collective-permute-start(bf16[64,1024]{1,0:T(8,128)(2,1)S(1)} %collective-permute-done.13), channel_id=1, source_target_pairs={{0,1},{1,2},{2,3},{3,4},{4,5},{5,6},{6,7},{7,8},{8,9},{9,10},{10,1... | collective-permute-start | bytes 393224 | tf_op jit(solution)/shard_map/ppermute | solution.py:72
  257.5 111.4 %all-reduce.2.cloned.1.call-start = ((), (), s32[]{:S(2)}) async-start(), calls=%async_computation.2 | async-start | bytes 524288 | tf_op jit(solution)/shard_map/psum | solution.py:103
  263.6 60.7 %collective-permute-start.20 = (bf16[128,4096]{0,1:T(8,128)(2,1)S(1)}, bf16[128,4096]{0,1:T(8,128)(2,1)S(1)}, u32[]{:S(2)}, u32[]{:S(2)}) collective-permute-start(bf16[128,4096]{0,1:T(8,128)(2,1)S(1)} %pad_maximum_fusion.1), channel_id=1, source_target_pairs={{8,0},{9,1},{10,2},{11,3},{12,4},{13,5},{14,6},{15,7},{0,8},{1,9},... | collective-permute-start | bytes 3145736 | tf_op jit(solution)/shard_map/ppermute | solution.py:15
  264.8 58.6 %collective-permute-start.21 = (bf16[128,1024]{1,0:T(8,128)(2,1)S(1)}, bf16[128,1024]{1,0:T(8,128)(2,1)S(1)}, u32[]{:S(2)}, u32[]{:S(2)}) collective-permute-start(bf16[128,1024]{1,0:T(8,128)(2,1)S(1)} %get-tuple-element.7), channel_id=1, source_target_pairs={{8,0},{9,1},{10,2},{11,3},{12,4},{13,5},{14,6},{15,7},{0,8},{1,9},... | collective-permute-start | bytes 786440 | tf_op jit(solution)/shard_map/ppermute | solution.py:15
  (66 other events, 649.7 us)
Sparse Core Ops, SparseCore 0:
  257.6 86.6 reduce-scatter.1
  346.5 22.2 all-reduce.1
